TPU v7x, 256 devices: a whole 4x4x8 slice. The times are simulated.
256 devices in a mesh: row: 16 (over z, core), col: 4 (over x), depth: 4 (over y).
Axes of the slice: x: 4, y: 4, z: 8, core: 2. Of those that a mesh axis runs over, the one named last changes fastest.
Arguments:
- diag_block: float32 [512, 512], P(('row', 'col')), may hold values from -40 to 60, as said below
- panel: float32 [16384, 512], P(('row', 'col'), 'depth'), may hold values from -1.2 to 1.2
- trailing: float32 [16384, 16384], P(('col', 'depth'), 'row'), may hold values from -6 to 6
Outputs:
- factor_diag: float32 [512, 512], P(('row', 'col'))
- factor_panel: float32 [16384, 512], P(('row', 'col'), 'depth')
- schur: float32 [16384, 16384], P(('col', 'depth'), 'row')
Inputs may be any that keep to these rules, and one draw needn't show every extreme that they name: `diag_block`: symmetric, with every eigenvalue 1 or more.
All inputs are finite; a program needn't handle non-finite values.
Results may differ from a plain program's by a relative error of at most 0.000071.
Values sent between devices are 32-bit elements; how exact they have to be, the bound alone decides.
A program may use at most 128 MiB of HBM per device.

v0:
```python
import jax
import jax.numpy as jnp
from jax import lax
from jax.sharding import PartitionSpec as P


def laid_out(pieces, dim):
    dims = list(pieces.shape[1:])
    dims[dim] *= pieces.shape[0]
    return jnp.moveaxis(pieces, 0, dim).reshape(dims)


def copy_for_each(array, axis):
    count = lax.axis_size(axis)
    return lax.all_to_all(
        jnp.broadcast_to(array[None], (count, *array.shape)), axis, 0, 0, tiled=True
    )


def collect(array, axis, dim):
    return laid_out(copy_for_each(array, axis), dim)


def padded_to(lines, count):
    spare = -lines.shape[0] % count
    if not spare:
        return lines
    return jnp.concatenate([lines, jnp.zeros((spare, *lines.shape[1:]), lines.dtype)])


def broadcast_by_parts(array, axis, root):
    lines = jnp.where(lax.axis_index(axis) == root, array, jnp.zeros_like(array)).reshape(
        -1, *array.shape[1:][-1:]
    )
    padded = padded_to(lines, lax.axis_size(axis))
    own = lax.psum_scatter(padded, axis, scatter_dimension=0, tiled=True)
    return lax.all_gather(own, axis, axis=0, tiled=True)[: len(lines)].reshape(array.shape)


def outer_rows(left, right):
    return lax.dot_general(
        left,
        right,
        (((1,), (1,)), ((), ())),
        precision=lax.Precision.HIGHEST,
        preferred_element_type=jnp.float32,
    )


def exact_dot(left, right):
    return jnp.dot(left, right, precision=lax.Precision.HIGHEST, preferred_element_type=jnp.float32)


def local(diag_block, panel, trailing):
    n_depth = lax.axis_size("depth")
    whole_diag = collect(diag_block, ("row", "col"), 0)
    lower = jnp.linalg.cholesky(whole_diag)
    ident = jnp.eye(lower.shape[0], dtype=jnp.float32)
    inverse = lax.linalg.triangular_solve(lower, ident, left_side=True, lower=True)
    inv_trans = inverse.T
    own_rows = diag_block.shape[0]
    factor_diag = lax.dynamic_slice_in_dim(
        lower, lax.axis_index(("row", "col")) * own_rows, own_rows, 0
    )
    layer = lax.axis_index("depth")
    col_index = lax.axis_index("col")
    width = panel.shape[1]
    full_panel = lax.all_gather(panel, "depth", axis=1, tiled=True)
    solved = exact_dot(full_panel, inv_trans)
    factor_panel = lax.dynamic_slice_in_dim(solved, layer * width, width, 1)
    row_full = lax.all_gather(solved, "col", axis=0, tiled=True)
    rows_out = trailing.shape[0]
    span = row_full.shape[0]
    block_index = col_index * n_depth + layer
    root = block_index * rows_out // span
    col_rows = broadcast_by_parts(row_full, "row", root)
    update = outer_rows(col_rows, row_full)
    schur = trailing - update
    return (factor_diag, factor_panel, schur)


def solution(mesh):
    in_specs = (P(("row", "col"), None), P(("row", "col"), "depth"), P(("col", "depth"), "row"))
    out_specs = (P(("row", "col"), None), P(("row", "col"), "depth"), P(("col", "depth"), "row"))
    return jax.shard_map(local, mesh=mesh, in_specs=in_specs, out_specs=out_specs, check_vma=False)
```

profile of v0, /device:TPU:1, one launch (start us, length us, event | category | flops | bytes accessed | tf_op | source)
XLA Modules:
  0.0 347.8 jit_solution(10400777857878367023)
XLA Ops:
  7.2 1.8 broadcast_in_dim.5
  9.0 13.0 %all-to-all-start = ((f32[64,8,512]{2,1,0:T(8,128)}), f32[64,8,512]{2,1,0:T(8,128)S(1)}, u32[]{:S(2)}, u32[]{:S(2)}) async-start(f32[64,8,512]{2,1,0:T(8,128)} %broadcast_in_dim.5), calls=%async_computation | async-start | bytes 2097152 | tf_op jit(solution)/shard_map/all_to_all | solution.py:15
  22.0 0.0 all-gather.3.cloned.1.call-start
  22.1 0.1 iota_compare_fusion
  22.2 0.1 fusion.18
  22.3 11.9 %all_gather.9 = f32[256,512]{1,0:T(8,128)} all-gather(f32[256,128]{1,0:T(8,128)S(1)} %copy-done.4), channel_id=1, replica_groups=mesh['row'=16,'col'=4,'depth'=4] {'depth'}, dimensions={1}, use_global_device_ids=true | all-gather | bytes 655360 | tf_op jit(solution)/shard_map/all_gather | solution.py:68
  34.2 15.6 %all-to-all-done = f32[64,8,512]{2,1,0:T(8,128)S(1)} async-done(((f32[64,8,512]{2,1,0:T(8,128)}), f32[64,8,512]{2,1,0:T(8,128)S(1)}, u32[]{:S(2)}, u32[]{:S(2)}) %all-to-all-start) | async-done | bytes 1048608 | tf_op jit(solution)/shard_map/all_to_all | solution.py:15
  49.8 0.3 copy.11
  50.1 0.2 fusion.8
  50.4 1.0 copy-done.1
  51.4 11.7 %cholesky.104 = f32[128,128]{1,0:T(8,128)S(1)} custom-call(f32[128,128]{1,0:T(8,128)S(1)} %cholesky.266), custom_call_target="Cholesky" | custom-call | tf_op jit(solution)/shard_map/jit(cholesky)/cholesky | solution.py:57
  63.1 9.8 %custom-call.30 = f32[1,128,128]{1,2,0:T(8,128)S(1)} custom-call(f32[1,128,128]{2,1,0:T(8,128)S(1)} %get-tuple-element.41), custom_call_target="InvertDiagBlocksLowerTriangular" | custom-call | tf_op jit(solution)/shard_map/jit(cholesky)/cholesky | solution.py:57
  72.9 0.1 cholesky.224
  73.0 1.2 constant_dynamic-update-slice_fusion.2
  74.3 1.3 convolution_subtract_fusion.4
  75.6 11.7 %cholesky.217 = f32[128,128]{1,0:T(8,128)S(1)} custom-call(f32[128,128]{1,0:T(8,128)S(1)} %cholesky.270), custom_call_target="Cholesky" | custom-call | tf_op jit(solution)/shard_map/jit(cholesky)/cholesky | solution.py:57
  87.3 9.9 %custom-call.31 = f32[1,128,128]{1,2,0:T(8,128)S(1)} custom-call(f32[1,128,128]{2,1,0:T(8,128)S(1)} %get-tuple-element.38), custom_call_target="InvertDiagBlocksLowerTriangular" | custom-call | tf_op jit(solution)/shard_map/jit(cholesky)/cholesky | solution.py:57
  97.3 0.3 convolution_dynamic-update-slice_fusion
  97.5 1.3 convolution_subtract_fusion.5
  98.8 11.7 %cholesky.238 = f32[128,128]{1,0:T(8,128)S(1)} custom-call(f32[128,128]{1,0:T(8,128)S(1)} %cholesky.275), custom_call_target="Cholesky" | custom-call | tf_op jit(solution)/shard_map/jit(cholesky)/cholesky | solution.py:57
  110.6 0.6 compare_reduce_fusion.1
  111.2 9.8 %custom-call.32 = f32[1,128,128]{1,2,0:T(8,128)S(1)} custom-call(f32[1,128,128]{2,1,0:T(8,128)S(1)} %get-tuple-element.35), custom_call_target="InvertDiagBlocksLowerTriangular" | custom-call | tf_op jit(solution)/shard_map/jit(cholesky)/cholesky | solution.py:57
  121.0 0.2 convolution_dynamic-update-slice_fusion.1
  121.2 1.2 convolution_subtract_fusion.6
  122.5 11.7 %cholesky.255 = f32[128,128]{1,0:T(8,128)S(1)} custom-call(f32[128,128]{1,0:T(8,128)S(1)} %convolution_subtract_fusion.6), custom_call_target="Cholesky" | custom-call | tf_op jit(solution)/shard_map/jit(cholesky)/cholesky | solution.py:57
  134.2 0.6 compare_reduce_fusion
  134.9 0.9 compare_reduce_fusion.2
  138.2 1.2 fusion.9
  139.4 10.4 %while.1 = (s32[]{:T(128)}, f32[512,512]{1,0:T(8,128)S(1)}, s32[4,2]{0,1:T(2,128)S(1)}, f32[4,128,128]{2,1,0:T(8,128)}, s32[]{:T(128)}) while((s32[]{:T(128)}, f32[512,512]{1,0:T(8,128)S(1)}, s32[4,2]{0,1:T(2,128)S(1)}, f32[4,128,128]{2,1,0:T(8,128)}, s32[]{:T(128)}) %tuple.35), condition=%wide.while_cond, body=%wide.while_body.sunk | while | flops 2 | bytes 132205 | solution.py:59
  139.4 0.1 constant_dynamic-slice_fusion.3
  139.5 0.5 fusion.51
  140.0 2.0 bitcast_dynamic-update-slice_fusion.2
  142.1 0.1 constant_dynamic-slice_fusion.3
  142.1 0.5 fusion.51
  142.6 2.0 bitcast_dynamic-update-slice_fusion.2
  144.7 0.1 constant_dynamic-slice_fusion.3
  144.7 0.5 fusion.51
  145.2 2.0 bitcast_dynamic-update-slice_fusion.2
  147.3 0.1 constant_dynamic-slice_fusion.3
  147.3 0.5 fusion.51
  147.8 2.0 bitcast_dynamic-update-slice_fusion.2
  149.8 40.1 %custom-call.33 = f32[4,128,128]{1,2,0:T(8,128)S(1)} custom-call(f32[4,128,128]{2,1,0:T(8,128)} %get-tuple-element.10), custom_call_target="InvertDiagBlocksLowerTriangular" | custom-call | tf_op jit(solution)/shard_map/triangular_solve | solution.py:59
  190.0 0.3 fusion.20
  190.3 0.4 convolution_subtract_fusion.2
  190.7 0.4 fusion.32
  191.1 0.4 convolution_subtract_fusion.1
  191.6 1.3 fusion.30
  192.8 0.6 convolution_subtract_fusion.3
  193.5 1.3 fusion.29
  194.7 1.8 fusion
  196.6 0.0 all-gather.3.cloned.1.call-update
  196.6 0.0 reduce-scatter.4.cloned.1.call-start
  196.7 30.4 %all-gather.3.cloned.1.call-done = f32[1024,512]{0,1:T(8,128)} async-done(((f32[256,512]{0,1:T(8,128)}), f32[1024,512]{0,1:T(8,128)}) %all-gather.3.cloned.1.call-update) | async-done | bytes 2097168 | tf_op jit(solution)/shard_map/all_gather | solution.py:71
  227.1 0.2 broadcast_select_fusion
  227.3 1.8 copy.14
  229.1 0.0 reduce-scatter.4.cloned.1.call-update
  229.1 0.0 all-gather.5.cloned.1.call-start
  229.2 58.4 %reduce-scatter.4.cloned.1.call-done = f32[64,512]{1,0:T(8,128)} async-done(((f32[1024,512]{1,0:T(8,128)}), f32[64,512]{1,0:T(8,128)}) %reduce-scatter.4.cloned.1.call-update) | async-done | bytes 131088 | tf_op jit(solution)/shard_map/reduce_scatter | solution.py:36
  287.6 0.0 all-gather.5.cloned.1.call-update
  287.6 0.9 dynamic-slice_bitcast_fusion
  288.5 0.8 copy.13
  289.3 1.3 constant_dynamic-slice_fusion.1
  290.6 40.3 %all-gather.5.cloned.1.call-done = f32[1024,512]{1,0:T(8,128)} async-done(((f32[64,512]{1,0:T(8,128)}), f32[1024,512]{1,0:T(8,128)}) %all-gather.5.cloned.1.call-update) | async-done | bytes 2097168 | tf_op jit(solution)/shard_map/all_gather | solution.py:37
  330.9 10.4 %convolution_subtract_fusion = f32[1024,1024]{1,0:T(8,128)} fusion(f32[1024,1024]{1,0:T(8,128)} %param.5, f32[1024,512]{1,0:T(8,128)} %all-gather.5.cloned.1.call-done, f32[1024,512]{0,1:T(8,128)S(1)} %copy-done), kind=kOutput, calls=%fused_computation.2 | convolution fusion | flops 6443499520 | bytes 12582912 | tf_op jit(solution)/shard_map/dot_general | solution.py:41
  (19 shorter events, 0.2 us)
Async XLA Ops:
  7.2 15.1 %copy-start.4 = (f32[256,128]{1,0:T(8,128)S(1)}, f32[256,128]{1,0:T(8,128)}, u32[]{:S(2)}) copy-start(f32[256,128]{1,0:T(8,128)} %param.4) | copy-start | bytes 393220
  9.0 40.8 %all-to-all-start = ((f32[64,8,512]{2,1,0:T(8,128)}), f32[64,8,512]{2,1,0:T(8,128)S(1)}, u32[]{:S(2)}, u32[]{:S(2)}) async-start(f32[64,8,512]{2,1,0:T(8,128)} %broadcast_in_dim.5), calls=%async_computation | async-start | bytes 2097152 | tf_op jit(solution)/shard_map/all_to_all | solution.py:15
  22.0 205.1 %all-gather.3.cloned.1.call-start = ((), (), s32[]{:S(2)}) async-start(), calls=%async_computation.2 | async-start | bytes 2621440 | tf_op jit(solution)/shard_map/all_gather | solution.py:71
  50.4 1.0 copy-start.1
  190.0 0.7 copy-start.3
  190.7 4.0 %copy-start.2 = (f32[256,512]{1,0:T(8,128)S(1)}, f32[256,512]{1,0:T(8,128)}, u32[]{:S(2)}) copy-start(f32[256,512]{1,0:T(8,128)} %all_gather.9) | copy-start | bytes 1572868
  196.6 90.9 %reduce-scatter.4.cloned.1.call-start = ((), (), s32[]{:S(2)}) async-start(), calls=%async_computation.4 | async-start | bytes 2228224 | tf_op jit(solution)/shard_map/reduce_scatter | solution.py:36
  229.1 101.8 %copy-start = (f32[1024,512]{0,1:T(8,128)S(1)}, f32[1024,512]{0,1:T(8,128)}, u32[]{:S(2)}) copy-start(f32[1024,512]{0,1:T(8,128)} %all-gather.3.cloned.1.call-done) | copy-start | bytes 6291460
  229.1 101.7 %all-gather.5.cloned.1.call-start = ((), (), s32[]{:S(2)}) async-start(), calls=%async_computation.3 | async-start | bytes 2228224 | tf_op jit(solution)/shard_map/all_gather | solution.py:37
Sparse Core Ops, SparseCore 0:
  196.7 30.3 all-gather.2
  230.2 57.2 reduce-scatter.3
  289.4 41.4 all-gather.4
where the time goes:
time: 348 us
  waiting for transfers between devices  145 us (42%)
  other arithmetic  121 us (35%)
  matrix products  22.4 us (6%)
  local copies, waits for them, and re-layouts  18.5 us (5%)
  between operations  16.6 us (5%)
  starting transfers between devices  13.1 us (4%)
  blocking collectives  11.9 us (3%)
    another operation x14, other arithmetic, local(): lower = jnp.linalg.cholesky(whole_diag)  78.7 us
    reduce_scatter x1, waiting for transfers between devices, broadcast_by_parts(): own = lax.psum_scatter(padded, axis, scatter_dimension=0, tiled=True)  58.4 us
    another operation x3, other arithmetic, local(): lax.linalg.triangular_solve(lower, ident, left_side=True, lower=True)  41.4 us
    all_gather x1, waiting for transfers between devices, broadcast_by_parts(): lax.all_gather(own, axis, axis=0, tiled=True)[:len(lines)]  40.3 us
    all_gather x1, waiting for transfers between devices, local(): row_full = lax.all_gather(solved, 'col', axis=0, tiled=True)  30.4 us
    all_to_all x1, waiting for transfers between devices, copy_for_each(): lax.all_to_all(jnp.broadcast_to(array[None], (count, *array.shape)), axis...  15.6 us
    all_to_all x1, starting transfers between devices, copy_for_each(): lax.all_to_all(jnp.broadcast_to(array[None], (count, *array.shape)), axis...  13 us
    all_gather x1, blocking collectives, local(): full_panel = lax.all_gather(panel, 'depth', axis=1, tiled=True)  11.9 us
  transfers between devices with their start and end apart: 4, of which 4 were waited for; matrix products, arithmetic and copies ran while one was open for 1% of the time, Pallas kernels for 0%

commit v1 on v0

--- a/solution.py
+++ b/solution.py
@@ -1,7 +1,103 @@
 import jax
 import jax.numpy as jnp
 from jax import lax
+from jax.experimental import pallas as pl
+from jax.experimental.pallas import tpu as pltpu
 from jax.sharding import PartitionSpec as P
+
+ORDER = 512
+BAND = 32
+
+
+def split3(x):
+    high = x.astype(jnp.bfloat16)
+    rest = x - high.astype(jnp.float32)
+    mid = rest.astype(jnp.bfloat16)
+    low = (rest - mid.astype(jnp.float32)).astype(jnp.bfloat16)
+    return high, mid, low
+
+
+def spread(rows, which):
+    return jnp.broadcast_to(rows[which : which + 1, :], (8, 128))
+
+
+def band_step(inv_ref, upper_ref, base, part):
+    start = pl.multiple_of(base + BAND * part, BAND)
+    group = pl.multiple_of(base, 128)
+    tiles = BAND // 8
+    here = inv_ref[pl.ds(start, BAND), pl.ds(group, 128)]
+    lane = lax.broadcasted_iota(jnp.int32, (8, 128), 1)
+    sub = lax.broadcasted_iota(jnp.int32, (8, 128), 0)
+    cols = []
+    for j in range(BAND):
+        first = j // 8
+        wide = jnp.broadcast_to(
+            here[8 * first :, BAND * part + j : BAND * part + j + 1], (BAND - 8 * first, 128)
+        )
+        cols.append([None] * first + [wide[8 * t : 8 * t + 8] for t in range(tiles - first)])
+    rows = []
+    for q in range(4):
+        strip = inv_ref[pl.ds(start, BAND), 128 * q : 128 * q + 128]
+        rows.append([strip[8 * t : 8 * t + 8] for t in range(tiles)])
+    rows.append(
+        [jnp.where(lane == sub + (BAND * part + 8 * t), 1.0, 0.0) for t in range(tiles)]
+    )
+    for j in range(BAND):
+        tj, sj = j // 8, j % 8
+        scale = lax.rsqrt(spread(cols[j][tj], sj))
+        factor = [None if col is None else col * scale for col in cols[j]]
+        for k in range(j + 1, BAND):
+            weight = spread(factor[k // 8], k % 8)
+            for t in range(k // 8, tiles):
+                cols[k][t] = cols[k][t] - factor[t] * weight
+        below = jnp.where(sub > sj, factor[tj], 0.0)
+        for strip in rows:
+            row = spread(strip[tj], sj) * scale
+            strip[tj] = jnp.where(sub == sj, row, strip[tj] - below * row)
+            for t in range(tj + 1, tiles):
+                strip[t] = strip[t] - factor[t] * row
+    lanes = lax.broadcasted_iota(jnp.int32, (BAND, 128), 1)
+    subs = lax.broadcasted_iota(jnp.int32, (BAND, 128), 0)
+    solved = [jnp.concatenate(strip, axis=0) for strip in rows]
+    right, whole = [], []
+    for q in range(4):
+        col = lanes + 128 * q
+        upper_ref[pl.ds(start, BAND), 128 * q : 128 * q + 128] = jnp.where(
+            col >= subs + start, solved[q], 0.0
+        )
+        right.append(jnp.where(col >= start + BAND, solved[q], 0.0))
+        whole.append(jnp.where((col >= start) & (col < start + BAND), solved[4], solved[q]))
+    right, whole = jnp.concatenate(right, axis=1), jnp.concatenate(whole, axis=1)
+    uh, um, ul = split3(right)
+    wh, wm, wl = split3(whole)
+    product = lax.dot_general(
+        jnp.concatenate([uh, uh, uh, um, um, ul, um, ul], axis=0),
+        jnp.concatenate([wh, wm, wl, wh, wm, wh, wl, wm], axis=0),
+        (((0,), (0,)), ((), ())),
+        preferred_element_type=jnp.float32,
+    )
+    col = lax.broadcasted_iota(jnp.int32, (ORDER, ORDER), 1)
+    inv_ref[...] = jnp.where((col >= start) & (col < start + BAND), 0.0, inv_ref[...]) - product
+    inv_ref[pl.ds(start, BAND), :] = whole
+
+
+def factor_kernel(diag_ref, inv_ref, upper_ref):
+    inv_ref[...] = diag_ref[...]
+
+    @pl.loop(0, ORDER // 128)
+    def _(block):
+        for part in range(128 // BAND):
+            band_step(inv_ref, upper_ref, block * 128, part)
+
+
+def factor_and_invert(diag):
+    return pl.pallas_call(
+        factor_kernel,
+        out_shape=(jax.ShapeDtypeStruct((ORDER, ORDER), jnp.float32),) * 2,
+        in_specs=[pl.BlockSpec(memory_space=pltpu.VMEM)],
+        out_specs=(pl.BlockSpec(memory_space=pltpu.VMEM),) * 2,
+        name="factor_and_invert",
+    )(diag)
 
 
 def laid_out(pieces, dim):
@@ -54,14 +150,12 @@
 def local(diag_block, panel, trailing):
     n_depth = lax.axis_size("depth")
     whole_diag = collect(diag_block, ("row", "col"), 0)
-    lower = jnp.linalg.cholesky(whole_diag)
-    ident = jnp.eye(lower.shape[0], dtype=jnp.float32)
-    inverse = lax.linalg.triangular_solve(lower, ident, left_side=True, lower=True)
+    inverse, upper = factor_and_invert(whole_diag)
     inv_trans = inverse.T
     own_rows = diag_block.shape[0]
     factor_diag = lax.dynamic_slice_in_dim(
-        lower, lax.axis_index(("row", "col")) * own_rows, own_rows, 0
-    )
+        upper, lax.axis_index(("row", "col")) * own_rows, own_rows, 1
+    ).T
     layer = lax.axis_index("depth")
     col_index = lax.axis_index("col")
     width = panel.shape[1]

time: 348 us -> 224 us (0.64)
  other arithmetic: 121 us -> 1.55 us
  Pallas kernels: 0 us -> 18.7 us
  local copies, waits for them, and re-layouts: 18.5 us -> 6.18 us
  matrix products: 22.4 us -> 13.5 us
    another operation x17 -> x0, other arithmetic: 120 us -> none  [the longest x14 78.7 us: local(): lower = jnp.linalg.cholesky(whole_diag)]
    pallas_call x0 -> x1, Pallas kernels: none -> 18.7 us  [factor_and_invert(): pl.pallas_call(factor_kernel, out_shape=(jax.ShapeDtypeStruct((ORDER, ORD...]
    another operation x17 -> x0, local copies, waits for them, and re-layouts: 10.5 us -> none
    another operation x13 -> x0, matrix products: 10.1 us -> none  [the longest x6 5.47 us: local(): lower = jnp.linalg.cholesky(whole_diag)]
  transfers between devices with their start and end apart: 4 -> 4, of which waited for: 4 -> 4; matrix products, arithmetic and copies ran while one was open for 1% -> 2% of each run, Pallas kernels for 0% -> 0%
where the time goes in v1:
time: 224 us
  waiting for transfers between devices  145 us (65%)
  Pallas kernels  18.7 us (8%)
  between operations  13.8 us (6%)
  matrix products  13.5 us (6%)
  starting transfers between devices  13.1 us (6%)
  blocking collectives  11.6 us (5%)
  local copies, waits for them, and re-layouts  6.18 us (3%)
    reduce_scatter x1, waiting for transfers between devices, broadcast_by_parts(): own = lax.psum_scatter(padded, axis, scatter_dimension=0, tiled=True)  59 us
    all_gather x1, waiting for transfers between devices, broadcast_by_parts(): lax.all_gather(own, axis, axis=0, tiled=True)[:len(lines)]  39.7 us
    all_gather x1, waiting for transfers between devices, local(): row_full = lax.all_gather(solved, 'col', axis=0, tiled=True)  30.4 us
    pallas_call x1, Pallas kernels, factor_and_invert(): pl.pallas_call(factor_kernel, out_shape=(jax.ShapeDtypeStruct((ORDER, ORD...  18.7 us
    all_to_all x1, waiting for transfers between devices, copy_for_each(): lax.all_to_all(jnp.broadcast_to(array[None], (count, *array.shape)), axis...  16.1 us
    all_to_all x1, starting transfers between devices, copy_for_each(): lax.all_to_all(jnp.broadcast_to(array[None], (count, *array.shape)), axis...  13 us
    all_gather x1, blocking collectives, local(): full_panel = lax.all_gather(panel, 'depth', axis=1, tiled=True)  11.6 us
    dot_general x1, matrix products, outer_rows(): lax.dot_general(left, right, (((1,), (1,)), ((), ())), precision=lax.Prec...  10.4 us
  transfers between devices with their start and end apart: 4, of which 4 were waited for; matrix products, arithmetic and copies ran while one was open for 2% of the time, Pallas kernels for 0%

profile of v1, /device:TPU:1, one launch (start us, length us, event | category | flops | bytes accessed | tf_op | source)
XLA Modules:
  0.0 223.8 jit_solution(10756088827595222601)
XLA Ops:
  7.2 0.0 copy-start.2
  7.2 1.8 broadcast_in_dim.4
  9.0 13.0 %all-to-all-start = ((f32[64,8,512]{2,1,0:T(8,128)}), f32[64,8,512]{2,1,0:T(8,128)S(1)}, u32[]{:S(2)}, u32[]{:S(2)}) async-start(f32[64,8,512]{2,1,0:T(8,128)} %broadcast_in_dim.4), calls=%async_computation | async-start | bytes 2097152 | tf_op jit(solution)/shard_map/all_to_all | solution.py:111
  22.0 0.0 all-gather.3.cloned.1.call-start
  22.1 0.0 copy-done.2
  22.1 11.6 %all_gather.9 = f32[256,512]{1,0:T(8,128)S(1)} all-gather(f32[256,128]{1,0:T(8,128)S(1)} %copy-done.2), channel_id=1, replica_groups=mesh['row'=16,'col'=4,'depth'=4] {'depth'}, dimensions={1}, use_global_device_ids=true | all-gather | bytes 655360 | tf_op jit(solution)/shard_map/all_gather | solution.py:162
  33.7 16.1 %all-to-all-done = f32[64,8,512]{2,1,0:T(8,128)S(1)} async-done(((f32[64,8,512]{2,1,0:T(8,128)}), f32[64,8,512]{2,1,0:T(8,128)S(1)}, u32[]{:S(2)}, u32[]{:S(2)}) %all-to-all-start) | async-done | bytes 1048608 | tf_op jit(solution)/shard_map/all_to_all | solution.py:111
  49.8 0.0 copy-start.1
  49.8 1.0 copy-done.1
  50.8 18.7 %factor_and_invert.1 = (f32[512,512]{1,0:T(8,128)}, f32[512,512]{1,0:T(8,128)}) custom-call(f32[512,512]{1,0:T(8,128)} %bitcast.7), custom_call_target="tpu_custom_call" | custom-call | tf_op jit(solution)/shard_map/factor_and_invert/pallas_call | solution.py:94
  69.5 3.1 %fusion = f32[256,512]{1,0:T(8,128)} fusion(f32[256,512]{1,0:T(8,128)S(1)} %all_gather.9, f32[512,512]{1,0:T(8,128)} %get-tuple-element.6), kind=kOutput, calls=%fused_computation.4 | convolution fusion | flops 805306368 | bytes 2097152 | tf_op jit(solution)/shard_map/dot_general | solution.py:147
  72.6 0.0 all-gather.3.cloned.1.call-update
  72.6 0.0 reduce-scatter.2.cloned.1.call-start
  72.7 30.4 %all-gather.3.cloned.1.call-done = f32[1024,512]{1,0:T(8,128)} async-done(((f32[256,512]{1,0:T(8,128)}), f32[1024,512]{1,0:T(8,128)}) %all-gather.3.cloned.1.call-update) | async-done | bytes 2097168 | tf_op jit(solution)/shard_map/all_gather | solution.py:165
  103.2 1.5 broadcast_select_fusion
  104.7 0.0 copy-start
  104.7 0.0 reduce-scatter.2.cloned.1.call-update
  104.7 0.0 all-gather.5.cloned.1.call-start
  104.8 59.0 %reduce-scatter.2.cloned.1.call-done = f32[64,512]{1,0:T(8,128)} async-done(((f32[1024,512]{1,0:T(8,128)}), f32[64,512]{1,0:T(8,128)}) %reduce-scatter.2.cloned.1.call-update) | async-done | bytes 131088 | tf_op jit(solution)/shard_map/reduce_scatter | solution.py:132
  163.8 0.0 all-gather.5.cloned.1.call-update
  163.8 1.1 dynamic-slice_bitcast_fusion
  164.9 0.7 copy.6
  165.6 1.6 constant_dynamic-slice_fusion
  167.2 39.7 %all-gather.5.cloned.1.call-done = f32[1024,512]{1,0:T(8,128)} async-done(((f32[64,512]{1,0:T(8,128)}), f32[1024,512]{1,0:T(8,128)}) %all-gather.5.cloned.1.call-update) | async-done | bytes 2097168 | tf_op jit(solution)/shard_map/all_gather | solution.py:133
  206.9 0.0 copy-done
  206.9 10.4 %convolution_subtract_fusion = f32[1024,1024]{1,0:T(8,128)} fusion(f32[1024,1024]{1,0:T(8,128)} %param.5, f32[1024,512]{1,0:T(8,128)} %all-gather.5.cloned.1.call-done, f32[1024,512]{1,0:T(8,128)S(1)} %copy-done), kind=kOutput, calls=%fused_computation | convolution fusion | flops 6443499520 | bytes 12582912 | tf_op jit(solution)/shard_map/dot_general | solution.py:137
Async XLA Ops:
  7.2 14.9 %copy-start.2 = (f32[256,128]{1,0:T(8,128)S(1)}, f32[256,128]{1,0:T(8,128)}, u32[]{:S(2)}) copy-start(f32[256,128]{1,0:T(8,128)} %param.4) | copy-start | bytes 393220
  9.0 40.8 %all-to-all-start = ((f32[64,8,512]{2,1,0:T(8,128)}), f32[64,8,512]{2,1,0:T(8,128)S(1)}, u32[]{:S(2)}, u32[]{:S(2)}) async-start(f32[64,8,512]{2,1,0:T(8,128)} %broadcast_in_dim.4), calls=%async_computation | async-start | bytes 2097152 | tf_op jit(solution)/shard_map/all_to_all | solution.py:111
  22.0 81.2 %all-gather.3.cloned.1.call-start = ((), (), s32[]{:S(2)}) async-start(), calls=%async_computation.2 | async-start | bytes 2621440 | tf_op jit(solution)/shard_map/all_gather | solution.py:165
  49.8 1.0 copy-start.1
  72.6 91.1 %reduce-scatter.2.cloned.1.call-start = ((), (), s32[]{:S(2)}) async-start(), calls=%async_computation.3 | async-start | bytes 2228224 | tf_op jit(solution)/shard_map/reduce_scatter | solution.py:132
  104.7 102.2 %copy-start = (f32[1024,512]{1,0:T(8,128)S(1)}, f32[1024,512]{1,0:T(8,128)}, u32[]{:S(2)}) copy-start(f32[1024,512]{1,0:T(8,128)} %all-gather.3.cloned.1.call-done) | copy-start | bytes 6291460
  104.7 102.2 %all-gather.5.cloned.1.call-start = ((), (), s32[]{:S(2)}) async-start(), calls=%async_computation.4 | async-start | bytes 2228224 | tf_op jit(solution)/shard_map/all_gather | solution.py:133
Sparse Core Ops, SparseCore 0:
  72.8 30.3 all-gather.2
  106.3 57.4 reduce-scatter.1
  165.6 41.2 all-gather.4

commit v2 on v1

--- a/solution.py
+++ b/solution.py
@@ -1,3 +1,5 @@
+import functools
+
 import jax
 import jax.numpy as jnp
 from jax import lax
@@ -81,96 +83,359 @@
     inv_ref[pl.ds(start, BAND), :] = whole
 
 
-def factor_kernel(diag_ref, inv_ref, upper_ref):
-    inv_ref[...] = diag_ref[...]
+MESH = pl.DeviceIdType.MESH
+F32 = jnp.float32
+BF16 = jnp.bfloat16
+SHIFTS = sorted(
+    [(i, j) for i in range(4) for j in range(4) if i or j],
+    key=lambda s: -(min(s[0], 4 - s[0]) + min(s[1], 4 - s[1])),
+)
+
+
+def exchange_kernel(
+    diag_ref,
+    panel_ref,
+    cols_ref,
+    rows_ref,
+    inv_out,
+    slab_ref,
+    gathered,
+    piece,
+    turned,
+    inv_ref,
+    upper_ref,
+    local_sem,
+    keep_sem,
+    z_send,
+    z_recv,
+    xy_send,
+    xy_recv,
+    pair_send,
+    pair_recv,
+    turn_send,
+    turn_recv,
+    rz_send,
+    rz_recv,
+    rp_send,
+    rp_recv,
+    c_send,
+    c_recv,
+    out_sem,
+):
+    row, c, d = lax.axis_index("row"), lax.axis_index("col"), lax.axis_index("depth")
+    z, k = row // 2, row % 2
+    block = 4 * c + d
+    turn_c, turn_d = row // 4, row % 4
+    fixed = block == row
+
+    def at(row_id, col_id, depth_id):
+        return {"row": row_id, "col": col_id, "depth": depth_id}
+
+    def remote(src, dst, send, recv, where):
+        return pltpu.make_async_remote_copy(
+            src_ref=src, dst_ref=dst, send_sem=send, recv_sem=recv,
+            device_id=where, device_id_type=MESH,
+        )
+
+    lane = pl.multiple_of(d * 128, 128)
+    load_diag = pltpu.make_async_copy(
+        diag_ref.at[:, pl.ds(lane, 128)], gathered.at[k, c, d, z], local_sem.at[0]
+    )
+    load_diag.start()
+    load_piece = pltpu.make_async_copy(panel_ref, piece, local_sem.at[1])
+    load_piece.start()
+
+    @pl.when(fixed)
+    def _():
+        pltpu.make_async_copy(panel_ref, turned, local_sem.at[2]).start()
+
+    barrier = pltpu.get_barrier_semaphore()
+
+    def greet(where):
+        pl.semaphore_signal(barrier, inc=1, device_id=where, device_id_type=MESH)
+
+    z_peers = [at(2 * ((z + s) % 8) + k, c, d) for s in range(8)]
+    xy_peers = [at(row, (c + i) % 4, (d + j) % 4) for i, j in SHIFTS]
+    partner = at(2 * z + 1 - k, c, d)
+    turn_peer = at(block, turn_c, turn_d)
+    for s in range(1, 8):
+        greet(z_peers[s])
+    for peer in xy_peers:
+        greet(peer)
+    greet(partner)
+
+    @pl.when(jnp.logical_not(fixed))
+    def _():
+        greet(turn_peer)
+
+    @pl.when(fixed)
+    def _():
+        pl.semaphore_wait(barrier, 23)
+
+    @pl.when(jnp.logical_not(fixed))
+    def _():
+        pl.semaphore_wait(barrier, 24)
+
+    load_diag.wait()
+    z_copies = [
+        remote(gathered.at[k, c, d, z], gathered.at[k, c, d, z], z_send.at[s], z_recv.at[s], z_peers[s])
+        for s in range(1, 8)
+    ]
+    for copy in z_copies:
+        copy.start()
+    load_piece.wait()
+
+    @pl.when(jnp.logical_not(fixed))
+    def _():
+        remote(piece, turned, turn_send, turn_recv, turn_peer).start()
+
+    keep_piece = pltpu.make_async_copy(piece, cols_ref.at[c, d], keep_sem.at[0])
+    keep_piece.start()
+    for s in range(1, 8):
+        from_z = (z - s + 8) % 8
+        remote(
+            gathered.at[k, c, d, from_z], gathered.at[k, c, d, from_z],
+            z_send.at[s], z_recv.at[s], z_peers[s],
+        ).wait_recv()
+
+    xy_copies = [
+        remote(gathered.at[k, c, d], gathered.at[k, c, d], xy_send.at[n], xy_recv.at[n], xy_peers[n])
+        for n in range(15)
+    ]
+    for copy in xy_copies:
+        copy.start()
+    pair_copies = [
+        remote(gathered.at[k, c, d], gathered.at[k, c, d], pair_send.at[15], pair_recv.at[15], partner)
+    ]
+    pair_copies[0].start()
+
+    @pl.when(fixed)
+    def _():
+        pltpu.make_async_copy(panel_ref, turned, local_sem.at[2]).wait()
+
+    @pl.when(jnp.logical_not(fixed))
+    def _():
+        remote(piece, turned, turn_send, turn_recv, turn_peer).wait_recv()
+
+    rz_copies = [
+        remote(turned, rows_ref.at[row], rz_send.at[s], rz_recv.at[s], z_peers[s])
+        for s in (4, 3, 5, 2, 6, 1, 7)
+    ]
+    for copy in rz_copies:
+        copy.start()
+    keep_turned = pltpu.make_async_copy(turned, rows_ref.at[row], keep_sem.at[1])
+    keep_turned.start()
+    rp_copies = [remote(turned, rows_ref.at[row], rp_send.at[0], rp_recv.at[0], partner)]
+    rp_copies[0].start()
+
+    for n in reversed(range(15)):
+        i, j = SHIFTS[n]
+        fc, fd = (c - i + 4) % 4, (d - j + 4) % 4
+        remote(
+            gathered.at[k, fc, fd], gathered.at[k, fc, fd], xy_send.at[n], xy_recv.at[n], xy_peers[n]
+        ).wait_recv()
+        copy = remote(
+            gathered.at[k, fc, fd], gathered.at[k, fc, fd], pair_send.at[n], pair_recv.at[n], partner
+        )
+        copy.start()
+        pair_copies.append(copy)
+
+    c_copies = [
+        remote(piece, cols_ref.at[c, d], c_send.at[n], c_recv.at[n], xy_peers[n]) for n in range(15)
+    ]
+    for copy in c_copies:
+        copy.start()
+    for n in range(16):
+        i, j = (0, 0) if n == 15 else SHIFTS[n]
+        fc, fd = (c - i + 4) % 4, (d - j + 4) % 4
+        remote(
+            gathered.at[1 - k, fc, fd], gathered.at[1 - k, fc, fd],
+            pair_send.at[n], pair_recv.at[n], partner,
+        ).wait_recv()
+
+    for fk in range(2):
+        for fc in range(4):
+            for fd in range(4):
+                for fz in range(8):
+                    first = (2 * fz + fk) * 32 + fc * 8
+                    inv_ref[first : first + 8, 128 * fd : 128 * fd + 128] = gathered[fk, fc, fd, fz]
+
+    def forward(s):
+        from_row = 2 * ((z - s + 8) % 8) + k
+        return (
+            remote(turned, rows_ref.at[from_row], rz_send.at[s], rz_recv.at[s], z_peers[s]),
+            remote(rows_ref.at[from_row], rows_ref.at[from_row], rp_send.at[s], rp_recv.at[s], partner),
+        )
 
     @pl.loop(0, ORDER // 128)
-    def _(block):
+    def _(step):
         for part in range(128 // BAND):
-            band_step(inv_ref, upper_ref, block * 128, part)
-
-
-def factor_and_invert(diag):
+            band_step(inv_ref, upper_ref, step * 128, part)
+
+    store_inv = pltpu.make_async_copy(inv_ref, inv_out, out_sem)
+    store_inv.start()
+    for s in range(1, 8):
+        arrived, onward = forward(s)
+        arrived.wait_recv()
+        onward.start()
+
+    mine = row * 4 + c
+    group = pl.multiple_of((mine // 16) * 128, 128)
+    upper_ref[:128, :] = upper_ref[:, pl.ds(group, 128)].T
+    slab_ref[...] = upper_ref[pl.ds(pl.multiple_of((mine % 16) * 8, 8), 8), :]
+
+    for n in range(15):
+        i, j = SHIFTS[n]
+        fc, fd = (c - i + 4) % 4, (d - j + 4) % 4
+        remote(piece, cols_ref.at[fc, fd], c_send.at[n], c_recv.at[n], xy_peers[n]).wait_recv()
+    for s in range(8):
+        from_row = 2 * ((z - s + 8) % 8) + 1 - k
+        remote(
+            rows_ref.at[from_row], rows_ref.at[from_row], rp_send.at[s], rp_recv.at[s], partner
+        ).wait_recv()
+    for s in range(1, 8):
+        forward(s)[1].wait_send()
+
+    @pl.when(jnp.logical_not(fixed))
+    def _():
+        remote(piece, turned, turn_send, turn_recv, turn_peer).wait_send()
+
+    for copy in z_copies + xy_copies + pair_copies + rz_copies + rp_copies + c_copies:
+        copy.wait_send()
+    keep_piece.wait()
+    keep_turned.wait()
+    store_inv.wait()
+
+
+def exchange_and_factor(diag_block, panel):
+    hbm = pl.BlockSpec(memory_space=pltpu.MemorySpace.HBM)
+    dma = pltpu.SemaphoreType.DMA
     return pl.pallas_call(
-        factor_kernel,
-        out_shape=(jax.ShapeDtypeStruct((ORDER, ORDER), jnp.float32),) * 2,
-        in_specs=[pl.BlockSpec(memory_space=pltpu.VMEM)],
-        out_specs=(pl.BlockSpec(memory_space=pltpu.VMEM),) * 2,
-        name="factor_and_invert",
-    )(diag)
-
-
-def laid_out(pieces, dim):
-    dims = list(pieces.shape[1:])
-    dims[dim] *= pieces.shape[0]
-    return jnp.moveaxis(pieces, 0, dim).reshape(dims)
-
-
-def copy_for_each(array, axis):
-    count = lax.axis_size(axis)
-    return lax.all_to_all(
-        jnp.broadcast_to(array[None], (count, *array.shape)), axis, 0, 0, tiled=True
+        exchange_kernel,
+        out_shape=(
+            jax.ShapeDtypeStruct((4, 4, 256, 128), F32),
+            jax.ShapeDtypeStruct((16, 256, 128), F32),
+            jax.ShapeDtypeStruct((ORDER, ORDER), F32),
+            jax.ShapeDtypeStruct((8, ORDER), F32),
+        ),
+        in_specs=[hbm, hbm],
+        out_specs=(hbm, hbm, hbm, pl.BlockSpec(memory_space=pltpu.VMEM)),
+        scratch_shapes=[
+            pltpu.VMEM((2, 4, 4, 8, 8, 128), F32),
+            pltpu.VMEM((256, 128), F32),
+            pltpu.VMEM((256, 128), F32),
+            pltpu.VMEM((ORDER, ORDER), F32),
+            pltpu.VMEM((ORDER, ORDER), F32),
+            dma((3,)),
+            dma((2,)),
+            dma((8,)),
+            dma((8,)),
+            dma((15,)),
+            dma((15,)),
+            dma((16,)),
+            dma((16,)),
+            dma,
+            dma,
+            dma((8,)),
+            dma((8,)),
+            dma((8,)),
+            dma((8,)),
+            dma((15,)),
+            dma((15,)),
+            dma,
+        ],
+        compiler_params=pltpu.CompilerParams(collective_id=0, has_side_effects=True),
+        name="exchange_and_factor",
+    )(diag_block, panel)
+
+
+def split2(x):
+    high = x.astype(BF16)
+    return high, (x - high.astype(F32)).astype(BF16)
+
+
+def dot_nt(left, right):
+    lh, ll = left
+    rh, rl = right
+    dims = (((1,), (1,)), ((), ()))
+    dot = functools.partial(lax.dot_general, dimension_numbers=dims, preferred_element_type=F32)
+    return dot(lh, rh) + dot(lh, rl) + dot(ll, rh)
+
+
+TILE = 256
+
+
+def update_kernel(
+    place_ref, cols_ref, rows_ref, inv_ref, slab_ref, trail_ref,
+    slab_out, panel_out, schur_ref, ih_ref, il_ref, sh_ref, sl_ref,
+):
+    step = pl.program_id(0)
+
+    def solve(pieces):
+        whole = jnp.concatenate(pieces, axis=1)
+        ph, pl_ = split2(whole)
+        left = dot_nt((ph[:, :256], pl_[:, :256]), (ih_ref[:256, :256], il_ref[:256, :256]))
+        right = dot_nt((ph, pl_), (ih_ref[256:, :], il_ref[256:, :]))
+        return jnp.concatenate([left, right], axis=1)
+
+    @pl.when(step == 0)
+    def _():
+        slab_out[...] = slab_ref[...]
+        ih_ref[...], il_ref[...] = split2(inv_ref[...])
+        for q in range(4):
+            part = solve([cols_ref[q, e] for e in range(4)])
+            sh, sl = split2(part)
+            sh_ref[256 * q : 256 * q + 256, :] = sh
+            sl_ref[256 * q : 256 * q + 256, :] = sl
+
+            @pl.when(place_ref[0] == q)
+            def _():
+                for e in range(4):
+
+                    @pl.when(place_ref[1] == e)
+                    def _():
+                        panel_out[...] = part[:, 128 * e : 128 * e + 128]
+
+    mine = split2(solve([rows_ref[4 * step + e] for e in range(4)]))
+    schur_ref[...] = trail_ref[...] - dot_nt(mine, (sh_ref[...], sl_ref[...]))
+
+
+def solve_and_update(cols, rows, inverse, slab, trailing):
+    place = jnp.stack([lax.axis_index("col"), lax.axis_index("depth")]).astype(jnp.int32)
+    whole = lambda *shape: pl.BlockSpec(
+        shape, lambda i, p: (0,) * len(shape), pipeline_mode=pl.Buffered(1)
     )
-
-
-def collect(array, axis, dim):
-    return laid_out(copy_for_each(array, axis), dim)
-
-
-def padded_to(lines, count):
-    spare = -lines.shape[0] % count
-    if not spare:
-        return lines
-    return jnp.concatenate([lines, jnp.zeros((spare, *lines.shape[1:]), lines.dtype)])
-
-
-def broadcast_by_parts(array, axis, root):
-    lines = jnp.where(lax.axis_index(axis) == root, array, jnp.zeros_like(array)).reshape(
-        -1, *array.shape[1:][-1:]
-    )
-    padded = padded_to(lines, lax.axis_size(axis))
-    own = lax.psum_scatter(padded, axis, scatter_dimension=0, tiled=True)
-    return lax.all_gather(own, axis, axis=0, tiled=True)[: len(lines)].reshape(array.shape)
-
-
-def outer_rows(left, right):
-    return lax.dot_general(
-        left,
-        right,
-        (((1,), (1,)), ((), ())),
-        precision=lax.Precision.HIGHEST,
-        preferred_element_type=jnp.float32,
-    )
-
-
-def exact_dot(left, right):
-    return jnp.dot(left, right, precision=lax.Precision.HIGHEST, preferred_element_type=jnp.float32)
+    tile = pl.BlockSpec((TILE, 1024), lambda i, p: (i, 0))
+    return pl.pallas_call(
+        update_kernel,
+        grid_spec=pltpu.PrefetchScalarGridSpec(
+            num_scalar_prefetch=1,
+            grid=(1024 // TILE,),
+            in_specs=[whole(4, 4, 256, 128), whole(16, 256, 128), whole(ORDER, ORDER), whole(8, ORDER), tile],
+            out_specs=(
+                pl.BlockSpec((8, ORDER), lambda i, p: (0, 0)),
+                pl.BlockSpec((256, 128), lambda i, p: (0, 0)),
+                tile,
+            ),
+            scratch_shapes=[
+                pltpu.VMEM((ORDER, ORDER), BF16),
+                pltpu.VMEM((ORDER, ORDER), BF16),
+                pltpu.VMEM((1024, ORDER), BF16),
+                pltpu.VMEM((1024, ORDER), BF16),
+            ],
+        ),
+        out_shape=(
+            jax.ShapeDtypeStruct((8, ORDER), F32),
+            jax.ShapeDtypeStruct((256, 128), F32),
+            jax.ShapeDtypeStruct((1024, 1024), F32),
+        ),
+        name="solve_and_update",
+    )(place, cols, rows, inverse, slab, trailing)
 
 
 def local(diag_block, panel, trailing):
-    n_depth = lax.axis_size("depth")
-    whole_diag = collect(diag_block, ("row", "col"), 0)
-    inverse, upper = factor_and_invert(whole_diag)
-    inv_trans = inverse.T
-    own_rows = diag_block.shape[0]
-    factor_diag = lax.dynamic_slice_in_dim(
-        upper, lax.axis_index(("row", "col")) * own_rows, own_rows, 1
-    ).T
-    layer = lax.axis_index("depth")
-    col_index = lax.axis_index("col")
-    width = panel.shape[1]
-    full_panel = lax.all_gather(panel, "depth", axis=1, tiled=True)
-    solved = exact_dot(full_panel, inv_trans)
-    factor_panel = lax.dynamic_slice_in_dim(solved, layer * width, width, 1)
-    row_full = lax.all_gather(solved, "col", axis=0, tiled=True)
-    rows_out = trailing.shape[0]
-    span = row_full.shape[0]
-    block_index = col_index * n_depth + layer
-    root = block_index * rows_out // span
-    col_rows = broadcast_by_parts(row_full, "row", root)
-    update = outer_rows(col_rows, row_full)
-    schur = trailing - update
-    return (factor_diag, factor_panel, schur)
+    cols, rows, inverse, slab = exchange_and_factor(diag_block, panel)
+    return solve_and_update(cols, rows, inverse, slab, trailing)
 
 
 def solution(mesh):

time: 224 us -> 74.6 us (0.33)
  waiting for transfers between devices: 145 us -> 0 us
  Pallas kernels: 18.7 us -> 72.3 us
  matrix products: 13.5 us -> 0 us
  between operations: 13.8 us -> 0.64 us
  starting transfers between devices: 13.1 us -> 0 us
  blocking collectives: 11.6 us -> 0 us
  local copies, waits for them, and re-layouts: 6.18 us -> 0 us
    all_gather x2 -> x0, waiting for transfers between devices: 70.1 us -> none  [the longest x1 39.7 us: broadcast_by_parts(): lax.all_gather(own, axis, axis=0, tiled=True)[:len(lines)]]
    reduce_scatter x1 -> x0, waiting for transfers between devices: 59 us -> none  [broadcast_by_parts(): own = lax.psum_scatter(padded, axis, scatter_dimension=0, tiled=True)]
    pallas_call x1 -> x2, Pallas kernels: 18.7 us -> 72.3 us  [the longest x1 56.7 us: exchange_and_factor(): pl.pallas_call(exchange_kernel, out_shape=(jax.ShapeDtypeStruct((4, 4, 25...]
    all_to_all x1 -> x0, waiting for transfers between devices: 16.1 us -> none  [copy_for_each(): lax.all_to_all(jnp.broadcast_to(array[None], (count, *array.shape)), axis...]
    dot_general x2 -> x0, matrix products: 13.5 us -> none  [the longest x1 10.4 us: outer_rows(): lax.dot_general(left, right, (((1,), (1,)), ((), ())), precision=lax.Prec...]
    all_to_all x1 -> x0, starting transfers between devices: 13 us -> none  [copy_for_each(): lax.all_to_all(jnp.broadcast_to(array[None], (count, *array.shape)), axis...]
    all_gather x1 -> x0, blocking collectives: 11.6 us -> none  [local(): full_panel = lax.all_gather(panel, 'depth', axis=1, tiled=True)]
  transfers between devices with their start and end apart: 4 -> 0, of which waited for: 4 -> 0; matrix products, arithmetic and copies ran while one was open for 2% -> 0% of each run, Pallas kernels for 0% -> 0%
where the time goes in v2:
time: 74.6 us; the launch traced here: 73.6 us
  Pallas kernels  72.3 us (97%)
    pallas_call x1, Pallas kernels, exchange_and_factor(): pl.pallas_call(exchange_kernel, out_shape=(jax.ShapeDtypeStruct((4, 4, 25...  56.7 us
    pallas_call x1, Pallas kernels, solve_and_update(): pl.pallas_call(update_kernel, grid_spec=pltpu.PrefetchScalarGridSpec(num_...  15.6 us

profile of v2, /device:TPU:1, one launch (start us, length us, event | category | flops | bytes accessed | tf_op | source)
XLA Modules:
  0.0 73.6 jit_solution(18337624320988436731)
XLA Ops:
  0.6 0.7 pad_add_fusion.place_ref
  1.3 56.7 %exchange_and_factor.1 = (f32[4,4,256,128]{3,2,1,0:T(8,128)}, f32[16,256,128]{2,1,0:T(8,128)}, f32[512,512]{1,0:T(8,128)}, f32[8,512]{1,0:T(8,128)}) custom-call(f32[8,512]{1,0:T(8,128)} %diag_ref.1, f32[256,128]{1,0:T(8,128)} %panel_ref.1), custom_call_target="tpu_custom_call" | custom-call | tf_op jit(solution)/shard_map/exchange_and_factor/pallas_call | solution.py:313
  58.0 15.6 %solve_and_update.1 = (f32[8,512]{1,0:T(8,128)}, f32[256,128]{1,0:T(8,128)}, f32[1024,1024]{1,0:T(8,128)}) custom-call(s32[2]{0:T(128)} %pad_add_fusion.place_ref, f32[4,4,256,128]{3,2,1,0:T(8,128)} %get-tuple-element.7.cols_ref, f32[16,256,128]{2,1,0:T(8,128)} %get-tuple-element.8.rows_ref, f32[512,512]{1,0:T(8,128)} %get-tuple-element.9.inv_ref, ...), custom_call_target="tpu_custom_call" | custom-call | tf_op jit(solution)/shard_map/solve_and_update/pallas_call | solution.py:409

commit v3 on v2

--- a/solution.py
+++ b/solution.py
@@ -91,6 +91,8 @@
     key=lambda s: -(min(s[0], 4 - s[0]) + min(s[1], 4 - s[1])),
 )
 
+FAR_FIRST = (4, 3, 5, 2, 6, 1, 7)
+
 
 def exchange_kernel(
     diag_ref,
@@ -156,9 +158,11 @@
 
     z_peers = [at(2 * ((z + s) % 8) + k, c, d) for s in range(8)]
     xy_peers = [at(row, (c + i) % 4, (d + j) % 4) for i, j in SHIFTS]
+    x_peers = [at(row, (c + i) % 4, d) for i in range(4)]
+    y_peers = [at(row, c, (d + j) % 4) for j in range(4)]
     partner = at(2 * z + 1 - k, c, d)
     turn_peer = at(block, turn_c, turn_d)
-    for s in range(1, 8):
+    for s in FAR_FIRST:
         greet(z_peers[s])
     for peer in xy_peers:
         greet(peer)
@@ -177,20 +181,32 @@
         pl.semaphore_wait(barrier, 24)
 
     load_diag.wait()
-    z_copies = [
-        remote(gathered.at[k, c, d, z], gathered.at[k, c, d, z], z_send.at[s], z_recv.at[s], z_peers[s])
-        for s in range(1, 8)
-    ]
-    for copy in z_copies:
+    sent = []
+
+    def start(copy):
         copy.start()
+        sent.append(copy)
+
+    for s in FAR_FIRST:
+        start(remote(
+            gathered.at[k, c, d, z], gathered.at[k, c, d, z], z_send.at[s], z_recv.at[s], z_peers[s]
+        ))
+
     load_piece.wait()
 
     @pl.when(jnp.logical_not(fixed))
     def _():
         remote(piece, turned, turn_send, turn_recv, turn_peer).start()
 
-    keep_piece = pltpu.make_async_copy(piece, cols_ref.at[c, d], keep_sem.at[0])
-    keep_piece.start()
+    halves = [piece.at[:128], piece.at[128:]]
+    own_slots = [cols_ref.at[0, d, c], cols_ref.at[1, c, d]]
+    keeps = [pltpu.make_async_copy(halves[h], own_slots[h], keep_sem.at[h]) for h in range(2)]
+    for h in range(2):
+        for s in (2, 1, 3):
+            peer = (x_peers, y_peers)[h][s]
+            start(remote(halves[h], own_slots[h], c_send.at[h, s], c_recv.at[h, s], peer))
+        keeps[h].start()
+
     for s in range(1, 8):
         from_z = (z - s + 8) % 8
         remote(
@@ -198,16 +214,13 @@
             z_send.at[s], z_recv.at[s], z_peers[s],
         ).wait_recv()
 
-    xy_copies = [
-        remote(gathered.at[k, c, d], gathered.at[k, c, d], xy_send.at[n], xy_recv.at[n], xy_peers[n])
-        for n in range(15)
-    ]
-    for copy in xy_copies:
-        copy.start()
-    pair_copies = [
-        remote(gathered.at[k, c, d], gathered.at[k, c, d], pair_send.at[15], pair_recv.at[15], partner)
-    ]
-    pair_copies[0].start()
+    for n in range(15):
+        start(remote(
+            gathered.at[k, c, d], gathered.at[k, c, d], xy_send.at[n], xy_recv.at[n], xy_peers[n]
+        ))
+    start(remote(
+        gathered.at[k, c, d], gathered.at[k, c, d], pair_send.at[15], pair_recv.at[15], partner
+    ))
 
     @pl.when(fixed)
     def _():
@@ -217,16 +230,11 @@
     def _():
         remote(piece, turned, turn_send, turn_recv, turn_peer).wait_recv()
 
-    rz_copies = [
-        remote(turned, rows_ref.at[row], rz_send.at[s], rz_recv.at[s], z_peers[s])
-        for s in (4, 3, 5, 2, 6, 1, 7)
-    ]
-    for copy in rz_copies:
-        copy.start()
-    keep_turned = pltpu.make_async_copy(turned, rows_ref.at[row], keep_sem.at[1])
+    for s in (2, 6, 1, 7):
+        start(remote(turned, rows_ref.at[row], rz_send.at[s], rz_recv.at[s], z_peers[s]))
+    keep_turned = pltpu.make_async_copy(turned, rows_ref.at[row], keep_sem.at[2])
     keep_turned.start()
-    rp_copies = [remote(turned, rows_ref.at[row], rp_send.at[0], rp_recv.at[0], partner)]
-    rp_copies[0].start()
+    start(remote(turned, rows_ref.at[row], rp_send.at[0], rp_recv.at[0], partner))
 
     for n in reversed(range(15)):
         i, j = SHIFTS[n]
@@ -234,18 +242,10 @@
         remote(
             gathered.at[k, fc, fd], gathered.at[k, fc, fd], xy_send.at[n], xy_recv.at[n], xy_peers[n]
         ).wait_recv()
-        copy = remote(
+        start(remote(
             gathered.at[k, fc, fd], gathered.at[k, fc, fd], pair_send.at[n], pair_recv.at[n], partner
-        )
-        copy.start()
-        pair_copies.append(copy)
-
-    c_copies = [
-        remote(piece, cols_ref.at[c, d], c_send.at[n], c_recv.at[n], xy_peers[n]) for n in range(15)
-    ]
-    for copy in c_copies:
-        copy.start()
-    for n in range(16):
+        ))
+    for n in reversed(range(16)):
         i, j = (0, 0) if n == 15 else SHIFTS[n]
         fc, fd = (c - i + 4) % 4, (d - j + 4) % 4
         remote(
@@ -253,6 +253,44 @@
             pair_send.at[n], pair_recv.at[n], partner,
         ).wait_recv()
 
+    def half_from(h, s):
+        if h == 0:
+            return cols_ref.at[0, d, (c - s + 4) % 4]
+        return cols_ref.at[1, c, (d - s + 4) % 4]
+
+    for h in range(2):
+        keeps[h].wait()
+        for s in range(1, 4):
+            slot = half_from(h, s)
+            remote(slot, slot, c_send.at[h, s], c_recv.at[h, s], partner).wait_recv()
+        line = cols_ref.at[h, (d, c)[h]]
+        for s in (2, 1, 3):
+            peer = (y_peers, x_peers)[h][s]
+            start(remote(line, line, c_send.at[h, 3 + s], c_recv.at[h, 3 + s], peer))
+
+    def from_row(s):
+        return 2 * ((z - s + 8) % 8) + k
+
+    def arrive(s):
+        slot = rows_ref.at[from_row(s)]
+        remote(slot, slot, rz_send.at[s], rz_recv.at[s], partner).wait_recv()
+
+    def pass_on(s):
+        slot = rows_ref.at[from_row(s)]
+        start(remote(slot, slot, rp_send.at[s], rp_recv.at[s], partner))
+
+    for s, side in ((2, 0), (6, 1)):
+        arrive(s)
+        slot = rows_ref.at[from_row(s)]
+        part = rows_ref.at[from_row(s), pl.ds(128 * side, 128)]
+        ahead, twice = ((1, 2), (7, 6))[side]
+        start(remote(part, part, rz_send.at[4 + 4 * side], rz_recv.at[4 + 4 * side], z_peers[twice]))
+        start(remote(slot, slot, rz_send.at[3 + 2 * side], rz_recv.at[3 + 2 * side], z_peers[ahead]))
+        pass_on(s)
+    for s in (1, 7):
+        arrive(s)
+        pass_on(s)
+
     for fk in range(2):
         for fc in range(4):
             for fd in range(4):
@@ -260,13 +298,6 @@
                     first = (2 * fz + fk) * 32 + fc * 8
                     inv_ref[first : first + 8, 128 * fd : 128 * fd + 128] = gathered[fk, fc, fd, fz]
 
-    def forward(s):
-        from_row = 2 * ((z - s + 8) % 8) + k
-        return (
-            remote(turned, rows_ref.at[from_row], rz_send.at[s], rz_recv.at[s], z_peers[s]),
-            remote(rows_ref.at[from_row], rows_ref.at[from_row], rp_send.at[s], rp_recv.at[s], partner),
-        )
-
     @pl.loop(0, ORDER // 128)
     def _(step):
         for part in range(128 // BAND):
@@ -274,35 +305,34 @@
 
     store_inv = pltpu.make_async_copy(inv_ref, inv_out, out_sem)
     store_inv.start()
-    for s in range(1, 8):
-        arrived, onward = forward(s)
-        arrived.wait_recv()
-        onward.start()
+    for s in (3, 5):
+        arrive(s)
+        pass_on(s)
+    for side in range(2):
+        part = rows_ref.at[from_row(4), pl.ds(128 * side, 128)]
+        sem = 4 + 4 * side
+        remote(part, part, rz_send.at[sem], rz_recv.at[sem], partner).wait_recv()
+    pass_on(4)
 
     mine = row * 4 + c
     group = pl.multiple_of((mine // 16) * 128, 128)
     upper_ref[:128, :] = upper_ref[:, pl.ds(group, 128)].T
     slab_ref[...] = upper_ref[pl.ds(pl.multiple_of((mine % 16) * 8, 8), 8), :]
 
-    for n in range(15):
-        i, j = SHIFTS[n]
-        fc, fd = (c - i + 4) % 4, (d - j + 4) % 4
-        remote(piece, cols_ref.at[fc, fd], c_send.at[n], c_recv.at[n], xy_peers[n]).wait_recv()
+    for h in range(2):
+        for s in range(1, 4):
+            line = cols_ref.at[h, ((d, c)[h] - s + 4) % 4]
+            remote(line, line, c_send.at[h, 3 + s], c_recv.at[h, 3 + s], partner).wait_recv()
     for s in range(8):
-        from_row = 2 * ((z - s + 8) % 8) + 1 - k
-        remote(
-            rows_ref.at[from_row], rows_ref.at[from_row], rp_send.at[s], rp_recv.at[s], partner
-        ).wait_recv()
-    for s in range(1, 8):
-        forward(s)[1].wait_send()
+        slot = rows_ref.at[2 * ((z - s + 8) % 8) + 1 - k]
+        remote(slot, slot, rp_send.at[s], rp_recv.at[s], partner).wait_recv()
 
     @pl.when(jnp.logical_not(fixed))
     def _():
         remote(piece, turned, turn_send, turn_recv, turn_peer).wait_send()
 
-    for copy in z_copies + xy_copies + pair_copies + rz_copies + rp_copies + c_copies:
+    for copy in sent:
         copy.wait_send()
-    keep_piece.wait()
     keep_turned.wait()
     store_inv.wait()
 
@@ -313,7 +343,7 @@
     return pl.pallas_call(
         exchange_kernel,
         out_shape=(
-            jax.ShapeDtypeStruct((4, 4, 256, 128), F32),
+            jax.ShapeDtypeStruct((2, 4, 4, 128, 128), F32),
             jax.ShapeDtypeStruct((16, 256, 128), F32),
             jax.ShapeDtypeStruct((ORDER, ORDER), F32),
             jax.ShapeDtypeStruct((8, ORDER), F32),
@@ -327,7 +357,7 @@
             pltpu.VMEM((ORDER, ORDER), F32),
             pltpu.VMEM((ORDER, ORDER), F32),
             dma((3,)),
-            dma((2,)),
+            dma((3,)),
             dma((8,)),
             dma((8,)),
             dma((15,)),
@@ -336,12 +366,12 @@
             dma((16,)),
             dma,
             dma,
+            dma((9,)),
+            dma((9,)),
             dma((8,)),
             dma((8,)),
-            dma((8,)),
-            dma((8,)),
-            dma((15,)),
-            dma((15,)),
+            dma((2, 7)),
+            dma((2, 7)),
             dma,
         ],
         compiler_params=pltpu.CompilerParams(collective_id=0, has_side_effects=True),
@@ -366,7 +396,7 @@
 
 
 def update_kernel(
-    place_ref, cols_ref, rows_ref, inv_ref, slab_ref, trail_ref,
+    cols_ref, rows_ref, inv_ref, slab_ref, trail_ref,
     slab_out, panel_out, schur_ref, ih_ref, il_ref, sh_ref, sl_ref,
 ):
     step = pl.program_id(0)
@@ -383,16 +413,18 @@
         slab_out[...] = slab_ref[...]
         ih_ref[...], il_ref[...] = split2(inv_ref[...])
         for q in range(4):
-            part = solve([cols_ref[q, e] for e in range(4)])
+            part = solve([
+                jnp.concatenate([cols_ref[0, e, q], cols_ref[1, q, e]], axis=0) for e in range(4)
+            ])
             sh, sl = split2(part)
             sh_ref[256 * q : 256 * q + 256, :] = sh
             sl_ref[256 * q : 256 * q + 256, :] = sl
 
-            @pl.when(place_ref[0] == q)
+            @pl.when(lax.axis_index("col") == q)
             def _():
                 for e in range(4):
 
-                    @pl.when(place_ref[1] == e)
+                    @pl.when(lax.axis_index("depth") == e)
                     def _():
                         panel_out[...] = part[:, 128 * e : 128 * e + 128]
 
@@ -401,20 +433,19 @@
 
 
 def solve_and_update(cols, rows, inverse, slab, trailing):
-    place = jnp.stack([lax.axis_index("col"), lax.axis_index("depth")]).astype(jnp.int32)
     whole = lambda *shape: pl.BlockSpec(
-        shape, lambda i, p: (0,) * len(shape), pipeline_mode=pl.Buffered(1)
+        shape, lambda i: (0,) * len(shape), pipeline_mode=pl.Buffered(1)
     )
-    tile = pl.BlockSpec((TILE, 1024), lambda i, p: (i, 0))
+    tile = pl.BlockSpec((TILE, 1024), lambda i: (i, 0))
     return pl.pallas_call(
         update_kernel,
         grid_spec=pltpu.PrefetchScalarGridSpec(
-            num_scalar_prefetch=1,
+            num_scalar_prefetch=0,
             grid=(1024 // TILE,),
-            in_specs=[whole(4, 4, 256, 128), whole(16, 256, 128), whole(ORDER, ORDER), whole(8, ORDER), tile],
+            in_specs=[whole(2, 4, 4, 128, 128), whole(16, 256, 128), whole(ORDER, ORDER), whole(8, ORDER), tile],
             out_specs=(
-                pl.BlockSpec((8, ORDER), lambda i, p: (0, 0)),
-                pl.BlockSpec((256, 128), lambda i, p: (0, 0)),
+                pl.BlockSpec((8, ORDER), lambda i: (0, 0)),
+                pl.BlockSpec((256, 128), lambda i: (0, 0)),
                 tile,
             ),
             scratch_shapes=[
@@ -430,7 +461,7 @@
             jax.ShapeDtypeStruct((1024, 1024), F32),
         ),
         name="solve_and_update",
-    )(place, cols, rows, inverse, slab, trailing)
+    )(cols, rows, inverse, slab, trailing)
 
 
 def local(diag_block, panel, trailing):

time: 74.6 us -> 71.9 us (0.964); the launches traced: 73.6 us -> 71.9 us
  Pallas kernels: 72.3 us -> 71.2 us
where the time goes in v3:
time: 71.9 us
  Pallas kernels  71.2 us (99%)
    pallas_call x1, Pallas kernels, exchange_and_factor(): pl.pallas_call(exchange_kernel, out_shape=(jax.ShapeDtypeStruct((2, 4, 4,...  56.3 us
    pallas_call x1, Pallas kernels, solve_and_update(): pl.pallas_call(update_kernel, grid_spec=pltpu.PrefetchScalarGridSpec(num_...  14.9 us

profile of v3, /device:TPU:1, one launch (start us, length us, event | category | flops | bytes accessed | tf_op | source)
XLA Modules:
  0.0 71.9 jit_solution(11815282232928319994)
XLA Ops:
  0.6 56.3 %exchange_and_factor.1 = (f32[2,4,4,128,128]{4,3,2,1,0:T(8,128)}, f32[16,256,128]{2,1,0:T(8,128)}, f32[512,512]{1,0:T(8,128)}, f32[8,512]{1,0:T(8,128)}) custom-call(f32[8,512]{1,0:T(8,128)} %diag_ref.1, f32[256,128]{1,0:T(8,128)} %panel_ref.1), custom_call_target="tpu_custom_call" | custom-call | tf_op jit(solution)/shard_map/exchange_and_factor/pallas_call | solution.py:343
  56.9 14.9 %solve_and_update.1 = (f32[8,512]{1,0:T(8,128)}, f32[256,128]{1,0:T(8,128)}, f32[1024,1024]{1,0:T(8,128)}) custom-call(f32[2,4,4,128,128]{4,3,2,1,0:T(8,128)} %get-tuple-element.7.cols_ref, f32[16,256,128]{2,1,0:T(8,128)} %get-tuple-element.8.rows_ref, f32[512,512]{1,0:T(8,128)} %get-tuple-element.9.inv_ref, f32[8,512]{1,0:T(8,128)} %get-tuple-element.10.slab_ref, ...), custom_call_target="tpu_custom_call" | custom-call | tf_op jit(solution)/shard_map/solve_and_update/pallas_call | solution.py:440

commit v4 on v3

--- a/solution.py
+++ b/solution.py
@@ -275,21 +275,28 @@
         slot = rows_ref.at[from_row(s)]
         remote(slot, slot, rz_send.at[s], rz_recv.at[s], partner).wait_recv()
 
-    def pass_on(s):
+    def onward(s):
         slot = rows_ref.at[from_row(s)]
-        start(remote(slot, slot, rp_send.at[s], rp_recv.at[s], partner))
-
-    for s, side in ((2, 0), (6, 1)):
+        return remote(slot, slot, rp_send.at[s], rp_recv.at[s], partner)
+
+    def near_rows_on(act):
+        for s, side in ((2, 0), (6, 1)):
+            slot = rows_ref.at[from_row(s)]
+            part = rows_ref.at[from_row(s), pl.ds(128 * side, 128)]
+            ahead, twice = ((1, 2), (7, 6))[side]
+            act(
+                s,
+                remote(part, part, rz_send.at[4 + 4 * side], rz_recv.at[4 + 4 * side], z_peers[twice]),
+                remote(slot, slot, rz_send.at[3 + 2 * side], rz_recv.at[3 + 2 * side], z_peers[ahead]),
+                onward(s),
+            )
+        for s in (1, 7):
+            act(s, onward(s))
+
+    def go_on(s, *copies):
         arrive(s)
-        slot = rows_ref.at[from_row(s)]
-        part = rows_ref.at[from_row(s), pl.ds(128 * side, 128)]
-        ahead, twice = ((1, 2), (7, 6))[side]
-        start(remote(part, part, rz_send.at[4 + 4 * side], rz_recv.at[4 + 4 * side], z_peers[twice]))
-        start(remote(slot, slot, rz_send.at[3 + 2 * side], rz_recv.at[3 + 2 * side], z_peers[ahead]))
-        pass_on(s)
-    for s in (1, 7):
-        arrive(s)
-        pass_on(s)
+        for copy in copies:
+            copy.start()
 
     for fk in range(2):
         for fc in range(4):
@@ -300,19 +307,29 @@
 
     @pl.loop(0, ORDER // 128)
     def _(step):
+        @pl.when(step == 1)
+        def _():
+            near_rows_on(go_on)
+
+        @pl.when(step == ORDER // 128 - 1)
+        def _():
+            for s in (3, 5):
+                arrive(s)
+                onward(s).start()
+            for side in range(2):
+                part = rows_ref.at[from_row(4), pl.ds(128 * side, 128)]
+                sem = 4 + 4 * side
+                remote(part, part, rz_send.at[sem], rz_recv.at[sem], partner).wait_recv()
+            onward(4).start()
+
         for part in range(128 // BAND):
             band_step(inv_ref, upper_ref, step * 128, part)
 
     store_inv = pltpu.make_async_copy(inv_ref, inv_out, out_sem)
     store_inv.start()
-    for s in (3, 5):
-        arrive(s)
-        pass_on(s)
-    for side in range(2):
-        part = rows_ref.at[from_row(4), pl.ds(128 * side, 128)]
-        sem = 4 + 4 * side
-        remote(part, part, rz_send.at[sem], rz_recv.at[sem], partner).wait_recv()
-    pass_on(4)
+    near_rows_on(lambda s, *copies: sent.extend(copies))
+    for s in (3, 5, 4):
+        sent.append(onward(s))
 
     mine = row * 4 + c
     group = pl.multiple_of((mine // 16) * 128, 128)
@@ -384,84 +401,80 @@
     return high, (x - high.astype(F32)).astype(BF16)
 
 
-def dot_nt(left, right):
-    lh, ll = left
-    rh, rl = right
-    dims = (((1,), (1,)), ((), ()))
-    dot = functools.partial(lax.dot_general, dimension_numbers=dims, preferred_element_type=F32)
-    return dot(lh, rh) + dot(lh, rl) + dot(ll, rh)
-
-
-TILE = 256
+def dot3(left, right, depth_axis):
+    (lh, ll), (rh, rl) = left, right
+    return lax.dot_general(
+        jnp.concatenate([lh, lh, ll], axis=1),
+        jnp.concatenate([rh, rl, rh], axis=depth_axis),
+        (((1,), (depth_axis,)), ((), ())),
+        preferred_element_type=F32,
+    )
 
 
 def update_kernel(
     cols_ref, rows_ref, inv_ref, slab_ref, trail_ref,
     slab_out, panel_out, schur_ref, ih_ref, il_ref, sh_ref, sl_ref,
 ):
-    step = pl.program_id(0)
-
-    def solve(pieces):
-        whole = jnp.concatenate(pieces, axis=1)
-        ph, pl_ = split2(whole)
-        left = dot_nt((ph[:, :256], pl_[:, :256]), (ih_ref[:256, :256], il_ref[:256, :256]))
-        right = dot_nt((ph, pl_), (ih_ref[256:, :], il_ref[256:, :]))
-        return jnp.concatenate([left, right], axis=1)
-
-    @pl.when(step == 0)
+    def cols_piece(q):
+        return split2(jnp.concatenate([
+            jnp.concatenate([cols_ref[0, e, q], cols_ref[1, q, e]], axis=0) for e in range(4)
+        ], axis=1))
+
+    @pl.when(pl.program_id(0) == 0)
     def _():
         slab_out[...] = slab_ref[...]
-        ih_ref[...], il_ref[...] = split2(inv_ref[...])
+        ih, il = split2(inv_ref[...])
         for q in range(4):
-            part = solve([
-                jnp.concatenate([cols_ref[0, e, q], cols_ref[1, q, e]], axis=0) for e in range(4)
-            ])
-            sh, sl = split2(part)
-            sh_ref[256 * q : 256 * q + 256, :] = sh
-            sl_ref[256 * q : 256 * q + 256, :] = sl
-
-            @pl.when(lax.axis_index("col") == q)
-            def _():
-                for e in range(4):
-
-                    @pl.when(lax.axis_index("depth") == e)
-                    def _():
-                        panel_out[...] = part[:, 128 * e : 128 * e + 128]
-
-    mine = split2(solve([rows_ref[4 * step + e] for e in range(4)]))
-    schur_ref[...] = trail_ref[...] - dot_nt(mine, (sh_ref[...], sl_ref[...]))
+            ph, pl_ = cols_piece(q)
+            top = dot3((ih[:256, :256], il[:256, :256]), (ph[:, :256], pl_[:, :256]), 1)
+            low = dot3((ih[256:], il[256:]), (ph, pl_), 1)
+            part = slice(256 * q, 256 * q + 256)
+            sh_ref[:, part], sl_ref[:, part] = split2(jnp.concatenate([top, low], axis=0))
+        ih_ref[...], il_ref[...] = split2(inv_ref[...].T)
+        first = pl.multiple_of(lax.axis_index("depth") * 128, 128)
+        panel_out[...] = dot3(
+            cols_piece(lax.axis_index("col")), split2(inv_ref[pl.ds(first, 128), :]), 1
+        )
+
+    ph, pl_ = split2(jnp.concatenate([rows_ref[0, e] for e in range(4)], axis=1))
+    left = dot3((ph[:, :256], pl_[:, :256]), (ih_ref[:256, :256], il_ref[:256, :256]), 0)
+    right = dot3((ph, pl_), (ih_ref[:, 256:], il_ref[:, 256:]), 0)
+    mine = split2(jnp.concatenate([left, right], axis=1))
+    schur_ref[...] = trail_ref[...] - dot3(mine, (sh_ref[...], sl_ref[...]), 0)
+
+
+TILE = 256
 
 
 def solve_and_update(cols, rows, inverse, slab, trailing):
-    whole = lambda *shape: pl.BlockSpec(
-        shape, lambda i: (0,) * len(shape), pipeline_mode=pl.Buffered(1)
-    )
+    def whole(*shape):
+        return pl.BlockSpec(shape, lambda i: (0,) * len(shape), pipeline_mode=pl.Buffered(1))
+
     tile = pl.BlockSpec((TILE, 1024), lambda i: (i, 0))
     return pl.pallas_call(
         update_kernel,
-        grid_spec=pltpu.PrefetchScalarGridSpec(
-            num_scalar_prefetch=0,
-            grid=(1024 // TILE,),
-            in_specs=[whole(2, 4, 4, 128, 128), whole(16, 256, 128), whole(ORDER, ORDER), whole(8, ORDER), tile],
-            out_specs=(
-                pl.BlockSpec((8, ORDER), lambda i: (0, 0)),
-                pl.BlockSpec((256, 128), lambda i: (0, 0)),
-                tile,
-            ),
-            scratch_shapes=[
-                pltpu.VMEM((ORDER, ORDER), BF16),
-                pltpu.VMEM((ORDER, ORDER), BF16),
-                pltpu.VMEM((1024, ORDER), BF16),
-                pltpu.VMEM((1024, ORDER), BF16),
-            ],
-        ),
+        grid=(1024 // TILE,),
+        in_specs=[
+            whole(2, 4, 4, 128, 128),
+            pl.BlockSpec((1, 4, TILE, 128), lambda i: (i, 0, 0, 0)),
+            whole(ORDER, ORDER),
+            whole(8, ORDER),
+            tile,
+        ],
+        out_specs=(whole(8, ORDER), whole(256, 128), tile),
         out_shape=(
             jax.ShapeDtypeStruct((8, ORDER), F32),
             jax.ShapeDtypeStruct((256, 128), F32),
             jax.ShapeDtypeStruct((1024, 1024), F32),
         ),
+        scratch_shapes=[
+            pltpu.VMEM((ORDER, ORDER), BF16),
+            pltpu.VMEM((ORDER, ORDER), BF16),
+            pltpu.VMEM((ORDER, 1024), BF16),
+            pltpu.VMEM((ORDER, 1024), BF16),
+        ],
         name="solve_and_update",
-    )(cols, rows, inverse, slab, trailing)
+    )(cols, rows.reshape(4, 4, TILE, 128), inverse, slab, trailing)
 
 
 def local(diag_block, panel, trailing):

time: 71.9 us -> 62 us (0.86)
  Pallas kernels: 71.2 us -> 60.7 us
    pallas_call x1, Pallas kernels: 56.3 us -> 49.8 us  [exchange_and_factor(): pl.pallas_call(exchange_kernel, out_shape=(jax.ShapeDtypeStruct((2, 4, 4,...]
    pallas_call x1, Pallas kernels: 14.9 us -> 11 us  [solve_and_update(): pl.pallas_call(update_kernel, grid=(1024 // TILE,), in_specs=[whole(2, 4,...]
where the time goes in v4:
time: 62 us; the launch traced here: 61.4 us
  Pallas kernels  60.7 us (98%)
  between operations  0.64 us (1%)
    pallas_call x1, Pallas kernels, exchange_and_factor(): pl.pallas_call(exchange_kernel, out_shape=(jax.ShapeDtypeStruct((2, 4, 4,...  49.8 us
    pallas_call x1, Pallas kernels, solve_and_update(): pl.pallas_call(update_kernel, grid=(1024 // TILE,), in_specs=[whole(2, 4,...  11 us

profile of v4, /device:TPU:1, one launch (start us, length us, event | category | flops | bytes accessed | tf_op | source)
XLA Modules:
  0.0 61.4 jit_solution(8661006953101199324)
XLA Ops:
  0.6 49.8 %exchange_and_factor.1 = (f32[2,4,4,128,128]{4,3,2,1,0:T(8,128)}, f32[16,256,128]{2,1,0:T(8,128)}, f32[512,512]{1,0:T(8,128)}, f32[8,512]{1,0:T(8,128)}) custom-call(f32[8,512]{1,0:T(8,128)} %diag_ref.1, f32[256,128]{1,0:T(8,128)} %panel_ref.1), custom_call_target="tpu_custom_call" | custom-call | tf_op jit(solution)/shard_map/exchange_and_factor/pallas_call | solution.py:360
  50.4 11.0 %solve_and_update.1 = (f32[8,512]{1,0:T(8,128)}, f32[256,128]{1,0:T(8,128)}, f32[1024,1024]{1,0:T(8,128)}) custom-call(f32[2,4,4,128,128]{4,3,2,1,0:T(8,128)} %get-tuple-element.7.cols_ref, f32[4,4,256,128]{3,2,1,0:T(8,128)} %bitcast.1, f32[512,512]{1,0:T(8,128)} %get-tuple-element.9.inv_ref, f32[8,512]{1,0:T(8,128)} %get-tuple-element.10.slab_ref, ...), custom_call_target="tpu_custom_call" | custom-call | tf_op jit(solution)/shard_map/solve_and_update/pallas_call | solution.py:454

commit v5 on v4

--- a/solution.py
+++ b/solution.py
@@ -9,21 +9,38 @@
 
 ORDER = 512
 BAND = 32
+F32 = jnp.float32
+BF16 = jnp.bfloat16
 
 
 def split3(x):
-    high = x.astype(jnp.bfloat16)
-    rest = x - high.astype(jnp.float32)
-    mid = rest.astype(jnp.bfloat16)
-    low = (rest - mid.astype(jnp.float32)).astype(jnp.bfloat16)
+    high = x.astype(BF16)
+    rest = x - high.astype(F32)
+    mid = rest.astype(BF16)
+    low = (rest - mid.astype(F32)).astype(BF16)
     return high, mid, low
+
+
+def left_parts(x):
+    h, m, l = split3(x)
+    return jnp.concatenate([h, h, h, m, m, l], axis=0)
+
+
+def right_parts(x):
+    h, m, l = split3(x)
+    return jnp.concatenate([h, m, l, h, m, h], axis=0)
+
+
+def dot_tn(left, right):
+    return lax.dot_general(left, right, (((0,), (0,)), ((), ())), preferred_element_type=F32)
 
 
 def spread(rows, which):
     return jnp.broadcast_to(rows[which : which + 1, :], (8, 128))
 
 
-def band_step(inv_ref, upper_ref, base, part):
+def band_step(inv_ref, upper_ref, step, part):
+    base = step * 128
     start = pl.multiple_of(base + BAND * part, BAND)
     group = pl.multiple_of(base, 128)
     tiles = BAND // 8
@@ -61,31 +78,50 @@
     lanes = lax.broadcasted_iota(jnp.int32, (BAND, 128), 1)
     subs = lax.broadcasted_iota(jnp.int32, (BAND, 128), 0)
     solved = [jnp.concatenate(strip, axis=0) for strip in rows]
-    right, whole = [], []
+    near = solved[0]
+    whole = []
     for q in range(4):
         col = lanes + 128 * q
         upper_ref[pl.ds(start, BAND), 128 * q : 128 * q + 128] = jnp.where(
             col >= subs + start, solved[q], 0.0
         )
-        right.append(jnp.where(col >= start + BAND, solved[q], 0.0))
         whole.append(jnp.where((col >= start) & (col < start + BAND), solved[4], solved[q]))
-    right, whole = jnp.concatenate(right, axis=1), jnp.concatenate(whole, axis=1)
-    uh, um, ul = split3(right)
-    wh, wm, wl = split3(whole)
-    product = lax.dot_general(
-        jnp.concatenate([uh, uh, uh, um, um, ul, um, ul], axis=0),
-        jnp.concatenate([wh, wm, wl, wh, wm, wh, wl, wm], axis=0),
-        (((0,), (0,)), ((), ())),
-        preferred_element_type=jnp.float32,
-    )
-    col = lax.broadcasted_iota(jnp.int32, (ORDER, ORDER), 1)
-    inv_ref[...] = jnp.where((col >= start) & (col < start + BAND), 0.0, inv_ref[...]) - product
+        if q:
+            near = jnp.where(step == q, solved[q], near)
+    whole = jnp.concatenate(whole, axis=1)
     inv_ref[pl.ds(start, BAND), :] = whole
+    rest = 128 - BAND * (part + 1)
+    if rest:
+        product = dot_tn(left_parts(near), right_parts(whole))
+        after = pl.multiple_of(start + BAND, BAND)
+        col = lax.broadcasted_iota(jnp.int32, (rest, ORDER), 1)
+        inv_ref[pl.ds(after, rest), :] = (
+            jnp.where((col >= start) & (col < start + BAND), 0.0, inv_ref[pl.ds(after, rest), :])
+            - product[128 - rest :, :]
+        )
+
+
+def group_step(inv_ref, upper_ref, parts_ref, step):
+    first = pl.multiple_of(step * 128, 128)
+    mine = inv_ref[pl.ds(first, 128), :]
+    col = lax.broadcasted_iota(jnp.int32, (128, ORDER), 1)
+    below = col <= lax.broadcasted_iota(jnp.int32, (128, ORDER), 0) + first
+    parts_ref[...] = right_parts(jnp.where(below | (col >= first + 128), mine, 0.0))
+    inv_ref[pl.ds(first, 128), :] = jnp.where(below, mine, 0.0)
+
+    @pl.loop(step + 1, 4)
+    def _(other):
+        at = pl.multiple_of(other * 128, 128)
+        product = dot_tn(
+            left_parts(upper_ref[pl.ds(first, 128), pl.ds(at, 128)]), parts_ref[...]
+        )
+        inv_ref[pl.ds(at, 128), :] = (
+            jnp.where((col >= first) & (col < first + 128), 0.0, inv_ref[pl.ds(at, 128), :])
+            - product
+        )
 
 
 MESH = pl.DeviceIdType.MESH
-F32 = jnp.float32
-BF16 = jnp.bfloat16
 SHIFTS = sorted(
     [(i, j) for i in range(4) for j in range(4) if i or j],
     key=lambda s: -(min(s[0], 4 - s[0]) + min(s[1], 4 - s[1])),
@@ -106,6 +142,7 @@
     turned,
     inv_ref,
     upper_ref,
+    parts_ref,
     local_sem,
     keep_sem,
     z_send,
@@ -214,13 +251,35 @@
             z_send.at[s], z_recv.at[s], z_peers[s],
         ).wait_recv()
 
-    for n in range(15):
-        start(remote(
-            gathered.at[k, c, d], gathered.at[k, c, d], xy_send.at[n], xy_recv.at[n], xy_peers[n]
-        ))
-    start(remote(
-        gathered.at[k, c, d], gathered.at[k, c, d], pair_send.at[15], pair_recv.at[15], partner
-    ))
+    early, late = pl.ds(0, 2), pl.ds(2, 6)
+
+    def across(n, part):
+        slot = gathered.at[k, c, d, (early, late)[part]]
+        return remote(slot, slot, xy_send.at[part, n], xy_recv.at[part, n], xy_peers[n])
+
+    def origin(n):
+        i, j = (0, 0) if n == 15 else SHIFTS[n]
+        return (c - i + 4) % 4, (d - j + 4) % 4
+
+    def crossed(n, part):
+        fc, fd = origin(n)
+        slot = gathered.at[k, fc, fd, (early, late)[part]]
+        remote(slot, slot, xy_send.at[part, n], xy_recv.at[part, n], partner).wait_recv()
+
+    def to_pair(n, part):
+        fc, fd = origin(n)
+        slot = gathered.at[k, fc, fd, (early, late)[part]]
+        return remote(slot, slot, pair_send.at[part, n], pair_recv.at[part, n], partner)
+
+    def from_pair(n, part):
+        fc, fd = origin(n)
+        slot = gathered.at[1 - k, fc, fd, (early, late)[part]]
+        remote(slot, slot, pair_send.at[part, n], pair_recv.at[part, n], partner).wait_recv()
+
+    for part in range(2):
+        for n in range(15):
+            start(across(n, part))
+        start(to_pair(15, part))
 
     @pl.when(fixed)
     def _():
@@ -237,21 +296,10 @@
     start(remote(turned, rows_ref.at[row], rp_send.at[0], rp_recv.at[0], partner))
 
     for n in reversed(range(15)):
-        i, j = SHIFTS[n]
-        fc, fd = (c - i + 4) % 4, (d - j + 4) % 4
-        remote(
-            gathered.at[k, fc, fd], gathered.at[k, fc, fd], xy_send.at[n], xy_recv.at[n], xy_peers[n]
-        ).wait_recv()
-        start(remote(
-            gathered.at[k, fc, fd], gathered.at[k, fc, fd], pair_send.at[n], pair_recv.at[n], partner
-        ))
+        crossed(n, 0)
+        start(to_pair(n, 0))
     for n in reversed(range(16)):
-        i, j = (0, 0) if n == 15 else SHIFTS[n]
-        fc, fd = (c - i + 4) % 4, (d - j + 4) % 4
-        remote(
-            gathered.at[1 - k, fc, fd], gathered.at[1 - k, fc, fd],
-            pair_send.at[n], pair_recv.at[n], partner,
-        ).wait_recv()
+        from_pair(n, 0)
 
     def half_from(h, s):
         if h == 0:
@@ -298,12 +346,19 @@
         for copy in copies:
             copy.start()
 
-    for fk in range(2):
-        for fc in range(4):
-            for fd in range(4):
-                for fz in range(8):
-                    first = (2 * fz + fk) * 32 + fc * 8
-                    inv_ref[first : first + 8, 128 * fd : 128 * fd + 128] = gathered[fk, fc, fd, fz]
+    def lay_out(planes):
+        for fk in range(2):
+            for fc in range(4):
+                for fd in range(4):
+                    for fz in planes:
+                        first = (2 * fz + fk) * 32 + fc * 8
+                        inv_ref[first : first + 8, 128 * fd : 128 * fd + 128] = gathered[fk, fc, fd, fz]
+
+    lay_out(range(2))
+
+    def store_group(step):
+        part = pl.ds(pl.multiple_of(step * 128, 128), 128)
+        return pltpu.make_async_copy(inv_ref.at[part], inv_out.at[part], out_sem.at[step])
 
     @pl.loop(0, ORDER // 128)
     def _(step):
@@ -323,10 +378,25 @@
             onward(4).start()
 
         for part in range(128 // BAND):
-            band_step(inv_ref, upper_ref, step * 128, part)
-
-    store_inv = pltpu.make_async_copy(inv_ref, inv_out, out_sem)
-    store_inv.start()
+            band_step(inv_ref, upper_ref, step, part)
+            if part == 1:
+
+                @pl.when(step == 0)
+                def _():
+                    for n in reversed(range(15)):
+                        crossed(n, 1)
+                        to_pair(n, 1).start()
+
+        @pl.when(step == 0)
+        def _():
+            for n in reversed(range(16)):
+                from_pair(n, 1)
+            lay_out(range(2, 8))
+
+        group_step(inv_ref, upper_ref, parts_ref, step)
+        store_group(step).start()
+
+    sent.extend(to_pair(n, 1) for n in range(15))
     near_rows_on(lambda s, *copies: sent.extend(copies))
     for s in (3, 5, 4):
         sent.append(onward(s))
@@ -351,7 +421,8 @@
     for copy in sent:
         copy.wait_send()
     keep_turned.wait()
-    store_inv.wait()
+    for step in range(ORDER // 128):
+        store_group(step).wait()
 
 
 def exchange_and_factor(diag_block, panel):
@@ -373,14 +444,15 @@
             pltpu.VMEM((256, 128), F32),
             pltpu.VMEM((ORDER, ORDER), F32),
             pltpu.VMEM((ORDER, ORDER), F32),
+            pltpu.VMEM((6 * 128, ORDER), BF16),
             dma((3,)),
             dma((3,)),
             dma((8,)),
             dma((8,)),
-            dma((15,)),
-            dma((15,)),
-            dma((16,)),
-            dma((16,)),
+            dma((2, 15)),
+            dma((2, 15)),
+            dma((2, 16)),
+            dma((2, 16)),
             dma,
             dma,
             dma((9,)),
@@ -389,7 +461,7 @@
             dma((8,)),
             dma((2, 7)),
             dma((2, 7)),
-            dma,
+            dma((4,)),
         ],
         compiler_params=pltpu.CompilerParams(collective_id=0, has_side_effects=True),
         name="exchange_and_factor",

time: 62 us -> 61 us (0.984)
  no operation moved by 1% of the time
where the time goes in v5:
time: 61 us; the launch traced here: 60.8 us
  Pallas kernels  60.2 us (99%)
  between operations  0.64 us (1%)
    pallas_call x1, Pallas kernels, exchange_and_factor(): pl.pallas_call(exchange_kernel, out_shape=(jax.ShapeDtypeStruct((2, 4, 4,...  49.2 us
    pallas_call x1, Pallas kernels, solve_and_update(): pl.pallas_call(update_kernel, grid=(1024 // TILE,), in_specs=[whole(2, 4,...  11 us

profile of v5, /device:TPU:1, one launch (start us, length us, event | category | flops | bytes accessed | tf_op | source)
XLA Modules:
  0.0 60.8 jit_solution(8756415470554944471)
XLA Ops:
  0.6 49.2 %exchange_and_factor.1 = (f32[2,4,4,128,128]{4,3,2,1,0:T(8,128)}, f32[16,256,128]{2,1,0:T(8,128)}, f32[512,512]{1,0:T(8,128)}, f32[8,512]{1,0:T(8,128)}) custom-call(f32[8,512]{1,0:T(8,128)} %diag_ref.1, f32[256,128]{1,0:T(8,128)} %panel_ref.1), custom_call_target="tpu_custom_call" | custom-call | tf_op jit(solution)/shard_map/exchange_and_factor/pallas_call | solution.py:431
  49.9 11.0 %solve_and_update.1 = (f32[8,512]{1,0:T(8,128)}, f32[256,128]{1,0:T(8,128)}, f32[1024,1024]{1,0:T(8,128)}) custom-call(f32[2,4,4,128,128]{4,3,2,1,0:T(8,128)} %get-tuple-element.7.cols_ref, f32[4,4,256,128]{3,2,1,0:T(8,128)} %bitcast.1, f32[512,512]{1,0:T(8,128)} %get-tuple-element.9.inv_ref, f32[8,512]{1,0:T(8,128)} %get-tuple-element.10.slab_ref, ...), custom_call_target="tpu_custom_call" | custom-call | tf_op jit(solution)/shard_map/solve_and_update/pallas_call | solution.py:526

commit v6 on v5

--- a/solution.py
+++ b/solution.py
@@ -109,16 +109,17 @@
     parts_ref[...] = right_parts(jnp.where(below | (col >= first + 128), mine, 0.0))
     inv_ref[pl.ds(first, 128), :] = jnp.where(below, mine, 0.0)
 
-    @pl.loop(step + 1, 4)
-    def _(other):
-        at = pl.multiple_of(other * 128, 128)
-        product = dot_tn(
-            left_parts(upper_ref[pl.ds(first, 128), pl.ds(at, 128)]), parts_ref[...]
-        )
-        inv_ref[pl.ds(at, 128), :] = (
-            jnp.where((col >= first) & (col < first + 128), 0.0, inv_ref[pl.ds(at, 128), :])
-            - product
-        )
+    for done in range(1, 4):
+
+        @pl.when(step == done - 1)
+        def _():
+            left = ORDER - 128 * done
+            product = dot_tn(
+                left_parts(upper_ref[128 * (done - 1) : 128 * done, 128 * done :]), parts_ref[...]
+            )
+            col = lax.broadcasted_iota(jnp.int32, (left, ORDER), 1)
+            gone = (col >= 128 * (done - 1)) & (col < 128 * done)
+            inv_ref[128 * done :, :] = jnp.where(gone, 0.0, inv_ref[128 * done :, :]) - product
 
 
 MESH = pl.DeviceIdType.MESH

time: 61 us -> 60.8 us (level)
  no operation moved by 1% of the time
where the time goes in v6:
time: 60.8 us; the launch traced here: 60.6 us
  Pallas kernels  60 us (99%)
  between operations  0.64 us (1%)
    pallas_call x1, Pallas kernels, exchange_and_factor(): pl.pallas_call(exchange_kernel, out_shape=(jax.ShapeDtypeStruct((2, 4, 4,...  49 us
    pallas_call x1, Pallas kernels, solve_and_update(): pl.pallas_call(update_kernel, grid=(1024 // TILE,), in_specs=[whole(2, 4,...  11 us

profile of v6, /device:TPU:1, one launch (start us, length us, event | category | flops | bytes accessed | tf_op | source)
XLA Modules:
  0.0 60.6 jit_solution(254864360752860518)
XLA Ops:
  0.6 49.0 %exchange_and_factor.1 = (f32[2,4,4,128,128]{4,3,2,1,0:T(8,128)}, f32[16,256,128]{2,1,0:T(8,128)}, f32[512,512]{1,0:T(8,128)}, f32[8,512]{1,0:T(8,128)}) custom-call(f32[8,512]{1,0:T(8,128)} %diag_ref.1, f32[256,128]{1,0:T(8,128)} %panel_ref.1), custom_call_target="tpu_custom_call" | custom-call | tf_op jit(solution)/shard_map/exchange_and_factor/pallas_call | solution.py:432
  49.7 11.0 %solve_and_update.1 = (f32[8,512]{1,0:T(8,128)}, f32[256,128]{1,0:T(8,128)}, f32[1024,1024]{1,0:T(8,128)}) custom-call(f32[2,4,4,128,128]{4,3,2,1,0:T(8,128)} %get-tuple-element.7.cols_ref, f32[4,4,256,128]{3,2,1,0:T(8,128)} %bitcast.1, f32[512,512]{1,0:T(8,128)} %get-tuple-element.9.inv_ref, f32[8,512]{1,0:T(8,128)} %get-tuple-element.10.slab_ref, ...), custom_call_target="tpu_custom_call" | custom-call | tf_op jit(solution)/shard_map/solve_and_update/pallas_call | solution.py:527
